TPU v7x, 256 devices: a whole 4x4x8 slice. The times are simulated.
256 devices in a mesh: band: 64 (over x, z, core), dir: 4 (over y).
Axes of the slice: x: 4, y: 4, z: 8, core: 2. Of those that a mesh axis runs over, the one named last changes fastest.
Arguments:
- visibilities: bfloat16 [128, 32, 2, 256, 256], P('band', 'dir'), as said below
- sky_model: bfloat16 [128, 32, 2, 256, 256], P('band', 'dir')
- rfi_flags: int32 [128, 8, 8], P('band'), may hold values from 0 to 1, as said below
- destination: int32 [128], P('band'), may hold values from 0 to 127, as said below
Outputs:
- delivered: float32 [128, 32, 2, 256], P('band', 'dir')
- coefficients: float32 [9, 32, 2, 256], P(None, 'dir')
- norm_values: float32 [2, 2], replicated
Inputs may be any that keep to these rules, and one draw needn't show every extreme that they name: `rfi_flags`: 1 marks a flagged baseline block; the share of flagged blocks tends to fall with the subband index. destination holds every row of 0 to 127 once. With the rows split into 64 aligned blocks of 2 rows, one row of block i goes to a row of block i + 1 and the other to a row of block i + 32, modulo 128 // 2. `visibilities`: visibilities follow the model under unknown station gains, with noise.
All inputs are finite; a program needn't handle non-finite values.
Results may differ from a plain program's by a relative error of at most 0.0003.
Values sent between devices are 32-bit elements; how exact they have to be, the bound alone decides.
No kernel may reach another device: no remote copies, remote signals or barrier semaphores. Data moves between devices by JAX's collectives and lax.ppermute only.
A program may use at most 128 MiB of HBM per device.

v0:
```python
import jax
import jax.numpy as jnp
from jax import lax
from jax.experimental import pallas as pl
from jax.experimental.pallas import tpu as pltpu
from jax.sharding import Mesh
from jax.sharding import PartitionSpec as P

BLOCK = 32
DEGREE = 8
SWEEPS = 4
BAND = ("band_0", "band_1", "band_2")
LOCAL = 2
DIRS = 8
STATIONS = 256
PAIRS = LOCAL * DIRS
ORDER = DEGREE + 1
CHUNK = 8
MSG_ROWS = 8
USED_ROWS = 6

f32 = jnp.float32
highest = lax.Precision.HIGHEST
penalty_share = 0.4


def iota(shape, dim):
    return lax.broadcasted_iota(jnp.int32, shape, dim)


def dot(a, b):
    return jnp.dot(a, b, precision=highest, preferred_element_type=f32)


def total(x):
    return jnp.sum(jnp.sum(x, axis=1, keepdims=True), axis=0, keepdims=True)


def band_weights(flags_ref):
    blocks = flags_ref.shape[-1]
    keep = [1.0 - flags_ref[f].astype(f32) for f in range(LOCAL)]
    return keep, [(1.0 + total(one)) / (1.0 + blocks * blocks) for one in keep]


def penalty_rows(weights):
    row = iota((PAIRS, STATIONS), 0)
    return jnp.where(row < DIRS, *(penalty_share * STATIONS * w for w in weights))


def row_sums(col_ref, part, j, rows, value):
    lane = part * PAIRS + j
    col_ref[rows, lane : lane + 1] = jnp.sum(
        value[:, :128] + value[:, 128:], axis=1, keepdims=True
    )


def products(re_ref, im_ref, sq_ref, gain_ref, col_ref):
    for j in range(PAIRS):
        g_re = jnp.broadcast_to(gain_ref[j : j + 1, :], (CHUNK, STATIONS))
        g_im = jnp.broadcast_to(gain_ref[PAIRS + j : PAIRS + j + 1, :], (CHUNK, STATIONS))
        mag = g_re * g_re + g_im * g_im
        for start in range(0, STATIONS, CHUNK):
            rows = slice(start, start + CHUNK)
            a_re = re_ref[j, rows, :]
            a_im = im_ref[j, rows, :]
            row_sums(col_ref, 0, j, rows, a_re * g_re - a_im * g_im)
            row_sums(col_ref, 1, j, rows, a_re * g_im + a_im * g_re)
            row_sums(col_ref, 2, j, rows, sq_ref[j, rows, :] * mag)
    return jnp.transpose(col_ref[...])[: 3 * PAIRS]


def updated(sums, target_re, target_im, pen):
    scale = sums[2 * PAIRS :] + pen
    return (
        (sums[:PAIRS] + pen * target_re) / scale,
        (sums[PAIRS : 2 * PAIRS] + pen * target_im) / scale,
    )


def sweeps(first, refs, gain_ref, col_ref, target_re, target_im, pen):
    def sweep(index, carry):
        new_re, new_im = updated(
            products(*refs, gain_ref, col_ref), target_re, target_im, pen
        )
        odd = index % 2 == 1
        gain_ref[:PAIRS] = jnp.where(odd, 0.5 * (new_re + gain_ref[:PAIRS]), new_re)
        gain_ref[PAIRS:] = jnp.where(odd, 0.5 * (new_im + gain_ref[PAIRS:]), new_im)
        return carry

    lax.fori_loop(first, SWEEPS, sweep, 0)


def write_message(gain_ref, msg_ref, extras):
    low = iota((DIRS, 128), 1) < 64
    for f in range(LOCAL):
        for part in range(2):
            start = part * PAIRS + f * DIRS
            for quarter in range(4):
                tile = gain_ref[start : start + DIRS, 128 * (quarter // 2) : 128 * (quarter // 2) + 128]
                if quarter % 2:
                    tile = pltpu.roll(tile, 64, 1)
                if extras is not None:
                    tile = jnp.where(low, tile, extras[f])
                msg_ref[pl.ds(quarter * 32 + 2 * part + f, DIRS, stride=4), :] = tile


def first_kernel(
    flags_ref, dest_ref, vis_ref, sky_ref, re_ref, im_ref, sq_ref, gain_ref, msg_ref,
    vis_buf, sky_buf, mask_ref, col_ref, sems,
):
    def copies(j):
        f, k = j // DIRS, j % DIRS
        return (
            pltpu.make_async_copy(vis_ref.at[f, k], vis_buf.at[j], sems.at[0, j]),
            pltpu.make_async_copy(sky_ref.at[f, k], sky_buf.at[j], sems.at[1, j]),
        )

    for j in range(PAIRS):
        for copy in copies(j):
            copy.start()
    blocks = flags_ref.shape[-1]
    keep, weights = band_weights(flags_ref)
    spread = ((iota((STATIONS, blocks), 0) >> 5) == iota((STATIONS, blocks), 1)).astype(f32)
    across = ((iota((blocks, STATIONS), 1) >> 5) == iota((blocks, STATIONS), 0)).astype(f32)
    apart = iota((STATIONS, STATIONS), 0) != iota((STATIONS, STATIONS), 1)
    for f in range(LOCAL):
        mask_ref[f] = jnp.where(apart, dot(dot(spread, keep[f]), across), 0.0)
    col_ref[...] = jnp.zeros(col_ref.shape, f32)
    for j in range(PAIRS):
        for copy in copies(j):
            copy.wait()
        for start in range(0, STATIONS, 16):
            rows = slice(start, start + 16)
            mask = mask_ref[j // DIRS, rows, :]
            data_re = vis_buf[j, 0, rows, :].astype(f32)
            data_im = vis_buf[j, 1, rows, :].astype(f32)
            model_re = mask * sky_buf[j, 0, rows, :].astype(f32)
            model_im = mask * sky_buf[j, 1, rows, :].astype(f32)
            a_re = model_re * data_re + model_im * data_im
            a_im = model_re * data_im - model_im * data_re
            sq = model_re * model_re + model_im * model_im
            re_ref[j, rows, :] = a_re
            im_ref[j, rows, :] = a_im
            sq_ref[j, rows, :] = sq
            row_sums(col_ref, 0, j, rows, a_re)
            row_sums(col_ref, 1, j, rows, a_im)
            row_sums(col_ref, 2, j, rows, sq)
    pen = penalty_rows(weights)
    ones, zeros = jnp.ones((PAIRS, STATIONS), f32), jnp.zeros((PAIRS, STATIONS), f32)
    sums = jnp.transpose(col_ref[...])[: 3 * PAIRS]
    gain_ref[:PAIRS], gain_ref[PAIRS:] = updated(sums, ones, zeros, pen)
    sweeps(1, (re_ref, im_ref, sq_ref), gain_ref, col_ref, ones, zeros, pen)
    lane = iota((DIRS, 128), 1)
    extras = [
        jnp.where(lane < 96, weights[f], dest_ref[f].astype(f32)) for f in range(LOCAL)
    ]
    write_message(gain_ref, msg_ref, extras)


def second_kernel(
    flags_ref, re_ref, im_ref, sq_ref, start_ref, back_ref, msg_ref, gain_ref, target_ref, col_ref
):
    low = iota((DIRS, 128), 1) < 64
    for f in range(LOCAL):
        for part in range(2):
            start = part * PAIRS + f * DIRS
            for half in range(2):
                first, second = (
                    back_ref[pl.ds(quarter * 32 + 2 * part + f, DIRS, stride=4), :]
                    for quarter in (2 * half, 2 * half + 1)
                )
                target_ref[start : start + DIRS, 128 * half : 128 * half + 128] = jnp.where(
                    low, first, pltpu.roll(second, 64, 1)
                )
    col_ref[...] = jnp.zeros(col_ref.shape, f32)
    pen = penalty_rows(band_weights(flags_ref)[1])
    target_re, target_im = target_ref[:PAIRS], target_ref[PAIRS:]
    gain_ref[...] = start_ref[...]
    sweeps(0, (re_ref, im_ref, sq_ref), gain_ref, col_ref, target_re, target_im, pen)
    write_message(gain_ref, msg_ref, None)


def chebyshev(abscissa):
    terms = [jnp.ones_like(abscissa), abscissa]
    for _ in range(2, ORDER):
        terms.append(2.0 * abscissa * terms[-1] - terms[-2])
    return terms


def basis_columns(bands):
    row, lane = iota((bands, 128), 0), iota((bands, 128), 1)
    out = jnp.zeros((bands, 128), f32)
    for c, term in enumerate(chebyshev((2.0 * row.astype(f32) + 1.0) / bands - 1.0)):
        out = jnp.where(lane == c, term, out)
    return out


def basis_rows(bands):
    row, lane = iota((16, bands), 0), iota((16, bands), 1)
    out = jnp.zeros((16, bands), f32)
    for c, term in enumerate(chebyshev((2.0 * lane.astype(f32) + 1.0) / bands - 1.0)):
        out = jnp.where(row == c, term, out)
    return out


def solve_kernel(x_ref, msg_ref, fresh_ref, coef_ref, inverse_ref, norm_ref):
    bands = x_ref.shape[0]
    low = iota((bands, 128), 1) < 64
    gains = jnp.where(low, x_ref[...], 0.0)
    weight = x_ref[:, 64:65]
    columns, rows = basis_columns(bands), basis_rows(bands)
    coef = dot(rows, weight * gains)
    gram = dot(rows, weight * columns)
    row = iota((16, 128), 0)
    inverse = (row == iota((16, 128), 1)).astype(f32)
    for i in range(ORDER):
        scale = 1.0 / gram[i : i + 1, i : i + 1]
        factor = jnp.where(row == i, 0.0, gram[:, i : i + 1])
        pivots = [m[i : i + 1, :] * scale for m in (coef, gram, inverse)]
        coef, gram, inverse = (
            jnp.where(row == i, pivot, m - factor * pivot)
            for m, pivot in zip((coef, gram, inverse), pivots)
        )
    fresh = dot(columns[:, :16], coef)
    msg_ref[...] = 2.0 * fresh - gains
    fresh_ref[...] = fresh
    coef_ref[...] = coef
    inverse_ref[...] = inverse
    start = jnp.where(lax.axis_index("band_2") == 0, 1.0, 0.0)
    primal = total(weight * (gains - fresh) ** 2)
    dual = total(jnp.where(low, weight * (fresh - start) ** 2, 0.0))
    lane = iota((8, 128), 1)
    norm_ref[...] = jnp.where(
        lane == 64, primal, jnp.where(lane == 65, dual, jnp.where(lane == 68, total(weight), 0.0))
    )


def finish_kernel(
    x_ref, target_ref, gain_ref, fresh_ref, coef_ref, inverse_ref, norm_ref, msg_ref,
    coef_buf, rows_buf,
):
    bands = x_ref.shape[0]
    owners = bands // 2
    low = iota((bands, 128), 1) < 64
    weight = x_ref[:, 64:65]
    gains = jnp.where(low, gain_ref[...], 0.0)
    columns, rows = basis_columns(bands), basis_rows(bands)
    change = dot(inverse_ref[:, :16], dot(rows, weight * (gains - target_ref[...])))
    step = dot(columns[:, :16], change)
    fresh = fresh_ref[...] + step
    primal = total(weight * (gains - fresh) ** 2)
    dual = total(weight * step * step)
    lane = iota((8, 128), 1)
    norms = jnp.where(lane == 66, primal, jnp.where(lane == 67, dual, norm_ref[...]))
    row = iota((16, 128), 0)
    coef_buf[...] = jnp.where(
        row == ORDER, pltpu.roll(norms[:1], 64, 1), coef_ref[...] + change
    )
    low = iota((8, 128), 1) < 64
    packed = jnp.where(
        low, coef_buf[pl.ds(0, 8, stride=2), :], pltpu.roll(coef_buf[pl.ds(1, 8, stride=2), :], 64, 1)
    )
    for r in range(USED_ROWS - 1):
        msg_ref[pl.ds(r, owners, stride=MSG_ROWS), :] = jnp.broadcast_to(
            packed[r : r + 1], (owners, 128)
        )
    lands = (x_ref[:, 96:97] == iota((bands, bands), 1).astype(f32)).astype(f32)
    rows_buf[...] = dot(jnp.transpose(lands), gains)
    for r in range(USED_ROWS, MSG_ROWS):
        msg_ref[pl.ds(r, owners, stride=MSG_ROWS), :] = jnp.zeros((owners, 128), f32)
    msg_ref[pl.ds(USED_ROWS - 1, owners, stride=MSG_ROWS), :] = jnp.where(
        iota((owners, 128), 1) < 64,
        rows_buf[pl.ds(0, owners, stride=2), :],
        pltpu.roll(rows_buf[pl.ds(1, owners, stride=2), :], 64, 1),
    )


def assemble_kernel(all_ref, delivered_ref, coef_ref, norm_ref):
    owners = all_ref.shape[0] // MSG_ROWS
    low = iota((16, 128), 1) < 64
    for r in range(USED_ROWS):
        for half in range(2):
            first, second = (
                all_ref[pl.ds(MSG_ROWS * 16 * quarter + r, 16, stride=MSG_ROWS), :]
                for quarter in (2 * half, 2 * half + 1)
            )
            tiles = (
                jnp.where(low, first, pltpu.roll(second, 64, 1)),
                jnp.where(low, pltpu.roll(first, 64, 1), second),
            )
            for odd in range(2):
                if r == USED_ROWS - 1:
                    out = delivered_ref.at[odd]
                elif 2 * r + odd < ORDER:
                    out = coef_ref.at[2 * r + odd]
                else:
                    continue
                for k in range(DIRS):
                    out[k, :, 128 * half : 128 * half + 128] = tiles[odd][2 * k : 2 * k + 2]
    norm_ref[...] = jnp.broadcast_to(
        jnp.sum(all_ref[pl.ds(ORDER // 2, owners, stride=MSG_ROWS), :], axis=0, keepdims=True),
        norm_ref.shape,
    )


def shape(*dims):
    return jax.ShapeDtypeStruct(dims, f32)


def call(kernel, outs, *args, scratch=(), in_specs=None, limit=8 << 20):
    in_specs = in_specs or [VMEM] * len(args)
    args = [
        pltpu.with_memory_space_constraint(arg, spec.memory_space)
        for arg, spec in zip(args, in_specs)
    ]
    return pl.pallas_call(
        kernel,
        out_shape=outs,
        in_specs=in_specs,
        scratch_shapes=list(scratch),
        compiler_params=pltpu.CompilerParams(vmem_limit_bytes=limit),
        name=kernel.__name__,
    )(*args)


VMEM = pl.BlockSpec(memory_space=pltpu.VMEM)
SMEM = pl.BlockSpec(memory_space=pltpu.SMEM)
HBM = pl.BlockSpec(memory_space=pltpu.HBM)


def exchange(message):
    return lax.all_to_all(message, BAND, split_axis=0, concat_axis=0, tiled=True)


def per_device(visibilities, sky_model, rfi_flags, destination):
    bands = LOCAL * lax.axis_size(BAND)
    columns = pltpu.VMEM((STATIONS, 128), f32)
    operator = pltpu.VMEM((PAIRS, STATIONS, STATIONS), f32)
    halves = pltpu.VMEM((PAIRS, 2, STATIONS, STATIONS), jnp.bfloat16)
    re, im, sq, gains, message = call(
        first_kernel,
        [operator, operator, operator, shape(2 * PAIRS, STATIONS), shape(bands, 128)],
        rfi_flags, destination, visibilities, sky_model,
        in_specs=[VMEM, SMEM, HBM, HBM],
        scratch=[
            halves, halves, pltpu.VMEM((LOCAL, STATIONS, STATIONS), f32), columns,
            pltpu.SemaphoreType.DMA((2, PAIRS)),
        ],
        limit=20 << 20,
    )
    operators = (re, im, sq)
    held = exchange(message)
    target, fresh, coef, inverse, norms = call(
        solve_kernel,
        [shape(bands, 128), shape(bands, 128), shape(16, 128), shape(16, 128), shape(8, 128)],
        held,
    )
    back = exchange(target)
    rows = pltpu.VMEM((2 * PAIRS, STATIONS), f32)
    message = call(
        second_kernel, shape(bands, 128), rfi_flags, *operators, gains, back,
        scratch=[rows, rows, columns],
    )
    message = call(
        finish_kernel, shape(MSG_ROWS * bands // LOCAL, 128),
        held, target, exchange(message), fresh, coef, inverse, norms,
        scratch=[pltpu.VMEM((16, 128), f32), pltpu.VMEM((bands, 128), f32)],
    )
    delivered, coefficients, norms = call(
        assemble_kernel,
        [
            shape(LOCAL, DIRS, 2, STATIONS), shape(ORDER, DIRS, 2, STATIONS), shape(8, 128),
        ],
        exchange(message),
    )
    count = lax.axis_size("dir")
    others = [
        lax.ppermute(norms, "dir", [(i, i ^ bit) for i in range(count)]) for bit in (1, 2, 3)
    ]
    sums = (norms + others[0]) + (others[1] + others[2])
    normalizer = (DIRS * count * 2.0 * STATIONS) * (norms[0, 68] / (bands // LOCAL))
    norm_values = jnp.sqrt(sums[0, 64:68].reshape(2, 2) / normalizer)
    return delivered, coefficients, norm_values


def solution(mesh):
    finer = Mesh(
        mesh.devices.reshape(4, 8, 2, mesh.shape["dir"]), ("band_0", "band_1", "band_2", "dir")
    )
    return jax.shard_map(
        per_device,
        mesh=finer,
        in_specs=(
            P(BAND, "dir", None, None, None),
            P(BAND, "dir", None, None, None),
            P(BAND, None, None),
            P(BAND),
        ),
        out_specs=(P(BAND, "dir", None, None), P(None, "dir", None, None), P()),
        check_vma=False,
    )
```

profile of v0, /device:TPU:6, one launch (start us, length us, event | category | flops | bytes accessed | tf_op | source)
XLA Modules:
  0.0 97.3 jit_solution(3995733430900588246)
XLA Ops:
  0.6 0.0 copy-start
  0.6 0.7 copy-done
  1.3 0.0 copy-start.1
  1.3 0.7 copy-done.1
  2.0 11.3 %first_kernel.1 = (f32[16,256,256]{2,1,0:T(8,128)S(1)}, f32[16,256,256]{2,1,0:T(8,128)S(1)}, f32[16,256,256]{2,1,0:T(8,128)S(1)}, f32[32,256]{1,0:T(8,128)S(1)}, f32[128,128]{1,0:T(8,128)S(1)}) custom-call(s32[2,8,8]{2,1,0:T(8,128)S(1)} %copy-done, s32[2]{0:T(128)S(1)} %copy-done.1, bf16[2,8,2,256,256]{4,3,2,1,0:T(8,128)(2,1)} %vis_ref.1, ...), custom_call_target="tpu_custom_call" | custom-call | tf_op jit(solution)/shard_map/first_kernel/pallas_call | solution.py:316
  13.3 19.7 %all_to_all.44 = f32[64,2,128]{2,1,0:T(2,128)S(1)} all-to-all(f32[64,2,128]{2,1,0:T(2,128)S(1)} %bitcast.17), channel_id=1, replica_groups=mesh['band_0'=4,'band_1'=8,'band_2'=2,'dir'=4] {'band_0','band_1','band_2'}, dimensions={0} | all-to-all | bytes 131072 | tf_op jit(solution)/shard_map/all_to_all | solution.py:332
  33.0 1.4 %solve_kernel.1 = (f32[128,128]{1,0:T(8,128)S(1)}, f32[128,128]{1,0:T(8,128)S(1)}, f32[16,128]{1,0:T(8,128)S(1)}, f32[16,128]{1,0:T(8,128)S(1)}, f32[8,128]{1,0:T(8,128)S(1)}) custom-call(f32[128,128]{1,0:T(8,128)S(1)} %bitcast.11), custom_call_target="tpu_custom_call" | custom-call | tf_op jit(solution)/shard_map/solve_kernel/pallas_call | solution.py:316
  34.5 13.6 %all_to_all.45 = f32[64,2,128]{2,1,0:T(2,128)S(1)} all-to-all(f32[64,2,128]{2,1,0:T(2,128)S(1)} %bitcast.15), channel_id=1, replica_groups=mesh['band_0'=4,'band_1'=8,'band_2'=2,'dir'=4] {'band_0','band_1','band_2'}, dimensions={0} | all-to-all | bytes 131072 | tf_op jit(solution)/shard_map/all_to_all | solution.py:332
  48.1 7.5 %second_kernel.1 = f32[128,128]{1,0:T(8,128)S(1)} custom-call(s32[2,8,8]{2,1,0:T(8,128)S(1)} %copy-done, f32[16,256,256]{2,1,0:T(8,128)S(1)} %get-tuple-element.18.re_ref, f32[16,256,256]{2,1,0:T(8,128)S(1)} %get-tuple-element.19.im_ref, f32[16,256,256]{2,1,0:T(8,128)S(1)} %get-tuple-element.20.sq_ref, f32[32,256]{1,0:T(8,128)S(1)} %get-tuple-element.21.start_ref, ...), custom_call_target="tpu_custom_call" | custom-call | tf_op jit(solution)/shard_map/second_kernel/pallas_call | solution.py:316
  55.5 13.6 %all_to_all.46 = f32[64,2,128]{2,1,0:T(2,128)S(1)} all-to-all(f32[64,2,128]{2,1,0:T(2,128)S(1)} %bitcast.14), channel_id=1, replica_groups=mesh['band_0'=4,'band_1'=8,'band_2'=2,'dir'=4] {'band_0','band_1','band_2'}, dimensions={0} | all-to-all | bytes 131072 | tf_op jit(solution)/shard_map/all_to_all | solution.py:332
  69.2 0.9 finish_kernel.1
  70.1 17.6 %all_to_all.47 = f32[64,8,128]{2,1,0:T(8,128)S(1)} all-to-all(f32[64,8,128]{2,1,0:T(8,128)S(1)} %bitcast.9), channel_id=1, replica_groups=mesh['band_0'=4,'band_1'=8,'band_2'=2,'dir'=4] {'band_0','band_1','band_2'}, dimensions={0} | all-to-all | bytes 524288 | tf_op jit(solution)/shard_map/all_to_all | solution.py:332
  87.7 0.8 assemble_kernel.1
  88.4 3.0 %collective-permute-start.2 = (f32[8,128]{1,0:T(8,128)S(1)}, f32[8,128]{1,0:T(8,128)S(1)}, u32[]{:S(2)}, u32[]{:S(2)}) collective-permute-start(f32[8,128]{1,0:T(8,128)S(1)} %get-tuple-element.28), channel_id=1, source_target_pairs={{0,3},{1,2},{2,1},{3,0},{4,7},{5,6},{6,5},{7,4},{8,11},{9,10},{10,... | collective-permute-start | bytes 12296 | tf_op jit(solution)/shard_map/ppermute | solution.py:378
  91.5 0.6 collective-permute-start.1
  92.1 0.5 collective-permute-start
  92.5 0.6 slice.7
  93.8 0.0 collective-permute-done.2
  93.8 2.8 %collective-permute-done.1 = f32[8,128]{1,0:T(8,128)S(1)} collective-permute-done((f32[8,128]{1,0:T(8,128)S(1)}, f32[8,128]{1,0:T(8,128)S(1)}, u32[]{:S(2)}, u32[]{:S(2)}) %collective-permute-start.1) | collective-permute-done | bytes 4128 | tf_op jit(solution)/shard_map/ppermute | solution.py:378
  96.6 0.0 collective-permute-done
  96.6 0.1 sqrt_reduce_fusion
  96.7 0.7 sqrt.7
  (1 shorter events, 0.0 us)
Async XLA Ops:
  0.6 0.7 copy-start
  1.3 0.7 copy-start.1
  88.4 5.3 %collective-permute-start.2 = (f32[8,128]{1,0:T(8,128)S(1)}, f32[8,128]{1,0:T(8,128)S(1)}, u32[]{:S(2)}, u32[]{:S(2)}) collective-permute-start(f32[8,128]{1,0:T(8,128)S(1)} %get-tuple-element.28), channel_id=1, source_target_pairs={{0,3},{1,2},{2,1},{3,0},{4,7},{5,6},{6,5},{7,4},{8,11},{9,10},{10,... | collective-permute-start | bytes 12296 | tf_op jit(solution)/shard_map/ppermute | solution.py:378
  91.5 5.1 %collective-permute-start.1 = (f32[8,128]{1,0:T(8,128)S(1)}, f32[8,128]{1,0:T(8,128)S(1)}, u32[]{:S(2)}, u32[]{:S(2)}) collective-permute-start(f32[8,128]{1,0:T(8,128)S(1)} %get-tuple-element.28), channel_id=1, source_target_pairs={{0,2},{1,3},{2,0},{3,1},{4,6},{5,7},{6,4},{7,5},{8,10},{9,11},{10,... | collective-permute-start | bytes 12296 | tf_op jit(solution)/shard_map/ppermute | solution.py:378
  92.1 4.5 %collective-permute-start = (f32[8,128]{1,0:T(8,128)S(1)}, f32[8,128]{1,0:T(8,128)S(1)}, u32[]{:S(2)}, u32[]{:S(2)}) collective-permute-start(f32[8,128]{1,0:T(8,128)S(1)} %get-tuple-element.28), channel_id=1, source_target_pairs={{0,1},{1,0},{2,3},{3,2},{4,5},{5,4},{6,7},{7,6},{8,9},{9,8},{10,11... | collective-permute-start | bytes 12296 | tf_op jit(solution)/shard_map/ppermute | solution.py:378
where the time goes:
time: 97.6 us; the launch traced here: 97.3 us
  blocking collectives  64.5 us (66%)
  Pallas kernels  21.9 us (22%)
  starting transfers between devices  4.09 us (4%)
  waiting for transfers between devices  2.79 us (3%)
  local copies, waits for them, and re-layouts  2.58 us (3%)
  between operations  1.33 us (1%)
    all_to_all x4, blocking collectives, exchange(): lax.all_to_all(message, BAND, split_axis=0, concat_axis=0, tiled=True)  64.5 us
    pallas_call x5, Pallas kernels, call(): pl.pallas_call(kernel, out_shape=outs, in_specs=in_specs, scratch_shapes=...  21.9 us
    ppermute x3, starting transfers between devices, per_device(): lax.ppermute(norms, 'dir', [(i, i ^ bit) for i in range(count)])  4.09 us
    ppermute x3, waiting for transfers between devices, per_device(): lax.ppermute(norms, 'dir', [(i, i ^ bit) for i in range(count)])  2.79 us
  transfers between devices with their start and end apart: 3, of which 1 were waited for; matrix products, arithmetic and copies ran while one was open for 1% of the time, Pallas kernels for 0%

commit v1 on v0

--- a/solution.py
+++ b/solution.py
@@ -16,10 +16,11 @@
 PAIRS = LOCAL * DIRS
 ORDER = DEGREE + 1
 CHUNK = 8
-MSG_ROWS = 8
-USED_ROWS = 6
+MSG_ROWS = 6
+AHEAD = 5
 
 f32 = jnp.float32
+bf16 = jnp.bfloat16
 highest = lax.Precision.HIGHEST
 penalty_share = 0.4
 
@@ -30,6 +31,10 @@
 
 def dot(a, b):
     return jnp.dot(a, b, precision=highest, preferred_element_type=f32)
+
+
+def matrix_dot(a, b):
+    return jnp.dot(a, b, preferred_element_type=f32)
 
 
 def total(x):
@@ -105,8 +110,8 @@
 
 
 def first_kernel(
-    flags_ref, dest_ref, vis_ref, sky_ref, re_ref, im_ref, sq_ref, gain_ref, msg_ref,
-    vis_buf, sky_buf, mask_ref, col_ref, sems,
+    flags_in, dest_in, vis_ref, sky_ref, re_ref, im_ref, sq_ref, gain_ref, pen_ref, msg_ref,
+    flags_ref, dest_ref, vis_buf, sky_buf, mask_ref, col_ref, sems,
 ):
     def copies(j):
         f, k = j // DIRS, j % DIRS
@@ -115,20 +120,29 @@
             pltpu.make_async_copy(sky_ref.at[f, k], sky_buf.at[j], sems.at[1, j]),
         )
 
-    for j in range(PAIRS):
+    flags_copy = pltpu.make_async_copy(flags_in, flags_ref, sems.at[0, PAIRS])
+    dest_copy = pltpu.make_async_copy(dest_in, dest_ref, sems.at[1, PAIRS])
+    flags_copy.start()
+    dest_copy.start()
+    for j in range(AHEAD):
         for copy in copies(j):
             copy.start()
+    flags_copy.wait()
     blocks = flags_ref.shape[-1]
     keep, weights = band_weights(flags_ref)
-    spread = ((iota((STATIONS, blocks), 0) >> 5) == iota((STATIONS, blocks), 1)).astype(f32)
-    across = ((iota((blocks, STATIONS), 1) >> 5) == iota((blocks, STATIONS), 0)).astype(f32)
+    spread = ((iota((STATIONS, blocks), 0) >> 5) == iota((STATIONS, blocks), 1)).astype(bf16)
+    across = ((iota((blocks, STATIONS), 1) >> 5) == iota((blocks, STATIONS), 0)).astype(bf16)
     apart = iota((STATIONS, STATIONS), 0) != iota((STATIONS, STATIONS), 1)
     for f in range(LOCAL):
-        mask_ref[f] = jnp.where(apart, dot(dot(spread, keep[f]), across), 0.0)
+        wide = matrix_dot(matrix_dot(spread, keep[f].astype(bf16)).astype(bf16), across)
+        mask_ref[f] = jnp.where(apart, wide, 0.0)
     col_ref[...] = jnp.zeros(col_ref.shape, f32)
     for j in range(PAIRS):
         for copy in copies(j):
             copy.wait()
+        if j + AHEAD < PAIRS:
+            for copy in copies(j + AHEAD):
+                copy.start()
         for start in range(0, STATIONS, 16):
             rows = slice(start, start + 16)
             mask = mask_ref[j // DIRS, rows, :]
@@ -146,11 +160,13 @@
             row_sums(col_ref, 1, j, rows, a_im)
             row_sums(col_ref, 2, j, rows, sq)
     pen = penalty_rows(weights)
+    pen_ref[...] = pen
     ones, zeros = jnp.ones((PAIRS, STATIONS), f32), jnp.zeros((PAIRS, STATIONS), f32)
     sums = jnp.transpose(col_ref[...])[: 3 * PAIRS]
     gain_ref[:PAIRS], gain_ref[PAIRS:] = updated(sums, ones, zeros, pen)
     sweeps(1, (re_ref, im_ref, sq_ref), gain_ref, col_ref, ones, zeros, pen)
     lane = iota((DIRS, 128), 1)
+    dest_copy.wait()
     extras = [
         jnp.where(lane < 96, weights[f], dest_ref[f].astype(f32)) for f in range(LOCAL)
     ]
@@ -158,7 +174,7 @@
 
 
 def second_kernel(
-    flags_ref, re_ref, im_ref, sq_ref, start_ref, back_ref, msg_ref, gain_ref, target_ref, col_ref
+    re_ref, im_ref, sq_ref, start_ref, pen_ref, back_ref, msg_ref, gain_ref, target_ref, col_ref
 ):
     low = iota((DIRS, 128), 1) < 64
     for f in range(LOCAL):
@@ -173,7 +189,7 @@
                     low, first, pltpu.roll(second, 64, 1)
                 )
     col_ref[...] = jnp.zeros(col_ref.shape, f32)
-    pen = penalty_rows(band_weights(flags_ref)[1])
+    pen = pen_ref[...]
     target_re, target_im = target_ref[:PAIRS], target_ref[PAIRS:]
     gain_ref[...] = start_ref[...]
     sweeps(0, (re_ref, im_ref, sq_ref), gain_ref, col_ref, target_re, target_im, pen)
@@ -260,25 +276,22 @@
     packed = jnp.where(
         low, coef_buf[pl.ds(0, 8, stride=2), :], pltpu.roll(coef_buf[pl.ds(1, 8, stride=2), :], 64, 1)
     )
-    for r in range(USED_ROWS - 1):
+    for r in range(MSG_ROWS - 1):
         msg_ref[pl.ds(r, owners, stride=MSG_ROWS), :] = jnp.broadcast_to(
             packed[r : r + 1], (owners, 128)
         )
     lands = (x_ref[:, 96:97] == iota((bands, bands), 1).astype(f32)).astype(f32)
     rows_buf[...] = dot(jnp.transpose(lands), gains)
-    for r in range(USED_ROWS, MSG_ROWS):
-        msg_ref[pl.ds(r, owners, stride=MSG_ROWS), :] = jnp.zeros((owners, 128), f32)
-    msg_ref[pl.ds(USED_ROWS - 1, owners, stride=MSG_ROWS), :] = jnp.where(
+    msg_ref[pl.ds(MSG_ROWS - 1, owners, stride=MSG_ROWS), :] = jnp.where(
         iota((owners, 128), 1) < 64,
         rows_buf[pl.ds(0, owners, stride=2), :],
         pltpu.roll(rows_buf[pl.ds(1, owners, stride=2), :], 64, 1),
     )
 
 
-def assemble_kernel(all_ref, delivered_ref, coef_ref, norm_ref):
-    owners = all_ref.shape[0] // MSG_ROWS
+def assemble_kernel(all_ref, delivered_ref, coef_ref):
     low = iota((16, 128), 1) < 64
-    for r in range(USED_ROWS):
+    for r in range(MSG_ROWS):
         for half in range(2):
             first, second = (
                 all_ref[pl.ds(MSG_ROWS * 16 * quarter + r, 16, stride=MSG_ROWS), :]
@@ -289,7 +302,7 @@
                 jnp.where(low, pltpu.roll(first, 64, 1), second),
             )
             for odd in range(2):
-                if r == USED_ROWS - 1:
+                if r == MSG_ROWS - 1:
                     out = delivered_ref.at[odd]
                 elif 2 * r + odd < ORDER:
                     out = coef_ref.at[2 * r + odd]
@@ -297,10 +310,24 @@
                     continue
                 for k in range(DIRS):
                     out[k, :, 128 * half : 128 * half + 128] = tiles[odd][2 * k : 2 * k + 2]
-    norm_ref[...] = jnp.broadcast_to(
-        jnp.sum(all_ref[pl.ds(ORDER // 2, owners, stride=MSG_ROWS), :], axis=0, keepdims=True),
-        norm_ref.shape,
-    )
+
+
+def norm_kernel(all_ref, norm_ref):
+    owners = all_ref.shape[0] // MSG_ROWS
+    sums = jnp.sum(all_ref[pl.ds(ORDER // 2, owners, stride=MSG_ROWS), :], axis=0, keepdims=True)
+    sums = jnp.broadcast_to(sums, (8, 128))
+    row = iota((8, 128), 0)
+    norm_ref[...] = jnp.where(
+        row == 0,
+        pltpu.roll(sums, 64, 1),
+        jnp.where(row == 1, pltpu.roll(sums, 62, 1), pltpu.roll(sums, 60, 1)),
+    )
+
+
+def total_kernel(own_ref, first_ref, second_ref, third_ref, out_ref):
+    sums = (own_ref[...] + second_ref[...]) + (first_ref[...] + third_ref[...])
+    scale = lax.axis_size(BAND) / (DIRS * lax.axis_size("dir") * 2.0 * STATIONS)
+    out_ref[...] = jnp.sqrt(scale * sums[:2, :2] / own_ref[2:3, :1])
 
 
 def shape(*dims):
@@ -324,7 +351,6 @@
 
 
 VMEM = pl.BlockSpec(memory_space=pltpu.VMEM)
-SMEM = pl.BlockSpec(memory_space=pltpu.SMEM)
 HBM = pl.BlockSpec(memory_space=pltpu.HBM)
 
 
@@ -337,18 +363,21 @@
     columns = pltpu.VMEM((STATIONS, 128), f32)
     operator = pltpu.VMEM((PAIRS, STATIONS, STATIONS), f32)
     halves = pltpu.VMEM((PAIRS, 2, STATIONS, STATIONS), jnp.bfloat16)
-    re, im, sq, gains, message = call(
+    *state, message = call(
         first_kernel,
-        [operator, operator, operator, shape(2 * PAIRS, STATIONS), shape(bands, 128)],
+        [
+            operator, operator, operator, shape(2 * PAIRS, STATIONS), shape(PAIRS, STATIONS),
+            shape(bands, 128),
+        ],
         rfi_flags, destination, visibilities, sky_model,
-        in_specs=[VMEM, SMEM, HBM, HBM],
+        in_specs=[HBM] * 4,
         scratch=[
+            pltpu.VMEM(rfi_flags.shape, jnp.int32), pltpu.SMEM(destination.shape, jnp.int32),
             halves, halves, pltpu.VMEM((LOCAL, STATIONS, STATIONS), f32), columns,
-            pltpu.SemaphoreType.DMA((2, PAIRS)),
+            pltpu.SemaphoreType.DMA((2, PAIRS + 1)),
         ],
         limit=20 << 20,
     )
-    operators = (re, im, sq)
     held = exchange(message)
     target, fresh, coef, inverse, norms = call(
         solve_kernel,
@@ -358,7 +387,7 @@
     back = exchange(target)
     rows = pltpu.VMEM((2 * PAIRS, STATIONS), f32)
     message = call(
-        second_kernel, shape(bands, 128), rfi_flags, *operators, gains, back,
+        second_kernel, shape(bands, 128), *state, back,
         scratch=[rows, rows, columns],
     )
     message = call(
@@ -366,20 +395,19 @@
         held, target, exchange(message), fresh, coef, inverse, norms,
         scratch=[pltpu.VMEM((16, 128), f32), pltpu.VMEM((bands, 128), f32)],
     )
-    delivered, coefficients, norms = call(
-        assemble_kernel,
-        [
-            shape(LOCAL, DIRS, 2, STATIONS), shape(ORDER, DIRS, 2, STATIONS), shape(8, 128),
-        ],
-        exchange(message),
-    )
+    everything = exchange(message.reshape(bands // LOCAL, 1, MSG_ROWS * 128)).reshape(-1, 128)
+    norms = call(norm_kernel, shape(8, 128), everything)
     count = lax.axis_size("dir")
     others = [
-        lax.ppermute(norms, "dir", [(i, i ^ bit) for i in range(count)]) for bit in (1, 2, 3)
+        lax.ppermute(norms, "dir", [(i, (i + step) % count) for i in range(count)])
+        for step in range(1, count)
     ]
-    sums = (norms + others[0]) + (others[1] + others[2])
-    normalizer = (DIRS * count * 2.0 * STATIONS) * (norms[0, 68] / (bands // LOCAL))
-    norm_values = jnp.sqrt(sums[0, 64:68].reshape(2, 2) / normalizer)
+    delivered, coefficients = call(
+        assemble_kernel,
+        [shape(LOCAL, DIRS, 2, STATIONS), shape(ORDER, DIRS, 2, STATIONS)],
+        everything,
+    )
+    norm_values = call(total_kernel, shape(2, 2), norms, *others)
     return delivered, coefficients, norm_values
 
 

time: 97.6 us -> 93.4 us (0.957)
  local copies, waits for them, and re-layouts: 2.58 us -> 0 us
  blocking collectives: 64.5 us -> 63.1 us
    all_to_all x4, blocking collectives: 64.5 us -> 63.1 us  [exchange(): lax.all_to_all(message, BAND, split_axis=0, concat_axis=0, tiled=True)]
    unnamed x4 -> x0, local copies, waits for them, and re-layouts: 1.34 us -> none
    pallas_call x5 -> x7, Pallas kernels: 21.9 us -> 21.7 us  [call(): pl.pallas_call(kernel, out_shape=outs, in_specs=in_specs, scratch_shapes=...]
  transfers between devices with their start and end apart: 3 -> 3, of which waited for: 1 -> 2; matrix products, arithmetic and copies ran while one was open for 1% -> 0% of each run, Pallas kernels for 0% -> 1%
where the time goes in v1:
time: 93.4 us; the launch traced here: 93.1 us
  blocking collectives  63.1 us (68%)
  Pallas kernels  21.7 us (23%)
  starting transfers between devices  4.62 us (5%)
  waiting for transfers between devices  3.07 us (3%)
    all_to_all x4, blocking collectives, exchange(): lax.all_to_all(message, BAND, split_axis=0, concat_axis=0, tiled=True)  63.1 us
    pallas_call x7, Pallas kernels, call(): pl.pallas_call(kernel, out_shape=outs, in_specs=in_specs, scratch_shapes=...  21.7 us
    ppermute x3, starting transfers between devices, per_device(): lax.ppermute(norms, 'dir', [(i, (i + step) % count) for i in range(count)])  4.62 us
    ppermute x3, waiting for transfers between devices, per_device(): lax.ppermute(norms, 'dir', [(i, (i + step) % count) for i in range(count)])  3.07 us
  transfers between devices with their start and end apart: 3, of which 2 were waited for; matrix products, arithmetic and copies ran while one was open for 0% of the time, Pallas kernels for 1%

profile of v1, /device:TPU:6, one launch (start us, length us, event | category | flops | bytes accessed | tf_op | source)
XLA Modules:
  0.0 93.1 jit_solution(5011978657356053572)
XLA Ops:
  0.6 10.6 %first_kernel.1 = (f32[16,256,256]{2,1,0:T(8,128)S(1)}, f32[16,256,256]{2,1,0:T(8,128)S(1)}, f32[16,256,256]{2,1,0:T(8,128)S(1)}, f32[32,256]{1,0:T(8,128)S(1)},...) custom-call(s32[2,8,8]{2,1,0:T(8,128)} %flags_in.1, s32[2]{0:T(128)} %dest_in.1, bf16[2,8,2,256,256]{4,3,2,1,0:T(8,128)(2,1)} %vis_ref.1, ...), custom_call_target="tpu_custom_call" | custom-call | tf_op jit(solution)/shard_map/first_kernel/pallas_call | solution.py:343
  11.2 19.7 %all_to_all.38 = f32[64,2,128]{2,1,0:T(2,128)S(1)} all-to-all(f32[64,2,128]{2,1,0:T(2,128)S(1)} %bitcast.17), channel_id=1, replica_groups=mesh['band_0'=4,'band_1'=8,'band_2'=2,'dir'=4] {'band_0','band_1','band_2'}, dimensions={0} | all-to-all | bytes 131072 | tf_op jit(solution)/shard_map/all_to_all | solution.py:358
  31.0 1.4 %solve_kernel.1 = (f32[128,128]{1,0:T(8,128)S(1)}, f32[128,128]{1,0:T(8,128)S(1)}, f32[16,128]{1,0:T(8,128)S(1)}, f32[16,128]{1,0:T(8,128)S(1)}, f32[8,128]{1,0:T(8,128)S(1)}) custom-call(f32[128,128]{1,0:T(8,128)S(1)} %bitcast.11), custom_call_target="tpu_custom_call" | custom-call | tf_op jit(solution)/shard_map/solve_kernel/pallas_call | solution.py:343
  32.4 13.6 %all_to_all.39 = f32[64,2,128]{2,1,0:T(2,128)S(1)} all-to-all(f32[64,2,128]{2,1,0:T(2,128)S(1)} %bitcast.15), channel_id=1, replica_groups=mesh['band_0'=4,'band_1'=8,'band_2'=2,'dir'=4] {'band_0','band_1','band_2'}, dimensions={0} | all-to-all | bytes 131072 | tf_op jit(solution)/shard_map/all_to_all | solution.py:358
  46.0 7.3 %second_kernel.1 = f32[128,128]{1,0:T(8,128)S(1)} custom-call(f32[16,256,256]{2,1,0:T(8,128)S(1)} %get-tuple-element.18.re_ref, f32[16,256,256]{2,1,0:T(8,128)S(1)} %get-tuple-element.19.im_ref, f32[16,256,256]{2,1,0:T(8,128)S(1)} %get-tuple-element.20.sq_ref, f32[32,256]{1,0:T(8,128)S(1)} %get-tuple-element.21.start_ref, ...), custom_call_target="tpu_custom_call" | custom-call | tf_op jit(solution)/shard_map/second_kernel/pallas_call | solution.py:343
  53.3 13.6 %all_to_all.40 = f32[64,2,128]{2,1,0:T(2,128)S(1)} all-to-all(f32[64,2,128]{2,1,0:T(2,128)S(1)} %bitcast.14), channel_id=1, replica_groups=mesh['band_0'=4,'band_1'=8,'band_2'=2,'dir'=4] {'band_0','band_1','band_2'}, dimensions={0} | all-to-all | bytes 131072 | tf_op jit(solution)/shard_map/all_to_all | solution.py:358
  66.9 0.9 finish_kernel.1
  67.8 16.1 %all_to_all.41 = f32[64,1,768]{2,1,0:T(1,128)S(1)} all-to-all(f32[64,1,768]{2,1,0:T(1,128)S(1)} %bitcast.10), channel_id=1, replica_groups=mesh['band_0'=4,'band_1'=8,'band_2'=2,'dir'=4] {'band_0','band_1','band_2'}, dimensions={0} | all-to-all | bytes 393216 | tf_op jit(solution)/shard_map/all_to_all | solution.py:358
  83.9 0.1 norm_kernel.1.own_ref
  84.0 3.0 %collective-permute-start.2 = (f32[8,128]{1,0:T(8,128)S(1)}, f32[8,128]{1,0:T(8,128)S(1)}, u32[]{:S(2)}, u32[]{:S(2)}) collective-permute-start(f32[8,128]{1,0:T(8,128)S(1)} %norm_kernel.1.own_ref), channel_id=1, source_target_pairs={{0,3},{1,0},{2,1},{3,2},{4,7},{5,4},{6,5},{7,6},{8,11},{9,8},{10,9... | collective-permute-start | bytes 12296 | tf_op jit(solution)/shard_map/ppermute | solution.py:402
  87.0 0.6 collective-permute-start.1
  87.7 1.0 %collective-permute-start = (f32[8,128]{1,0:T(8,128)S(1)}, f32[8,128]{1,0:T(8,128)S(1)}, u32[]{:S(2)}, u32[]{:S(2)}) collective-permute-start(f32[8,128]{1,0:T(8,128)S(1)} %norm_kernel.1.own_ref), channel_id=1, source_target_pairs={{0,1},{1,2},{2,3},{3,0},{4,5},{5,6},{6,7},{7,4},{8,9},{9,10},{10,1... | collective-permute-start | bytes 12296 | tf_op jit(solution)/shard_map/ppermute | solution.py:402
  88.6 0.8 assemble_kernel.1
  89.4 0.0 collective-permute-done.2.third_ref
  89.4 2.7 %collective-permute-done.1.second_ref = f32[8,128]{1,0:T(8,128)S(1)} collective-permute-done((f32[8,128]{1,0:T(8,128)S(1)}, f32[8,128]{1,0:T(8,128)S(1)}, u32[]{:S(2)}, u32[]{:S(2)}) %collective-permute-start.1) | collective-permute-done | bytes 4128 | tf_op jit(solution)/shard_map/ppermute | solution.py:402
  92.1 0.3 collective-permute-done.first_ref
  92.5 0.6 total_kernel.1
Async XLA Ops:
  84.0 5.4 %collective-permute-start.2 = (f32[8,128]{1,0:T(8,128)S(1)}, f32[8,128]{1,0:T(8,128)S(1)}, u32[]{:S(2)}, u32[]{:S(2)}) collective-permute-start(f32[8,128]{1,0:T(8,128)S(1)} %norm_kernel.1.own_ref), channel_id=1, source_target_pairs={{0,3},{1,0},{2,1},{3,2},{4,7},{5,4},{6,5},{7,6},{8,11},{9,8},{10,9... | collective-permute-start | bytes 12296 | tf_op jit(solution)/shard_map/ppermute | solution.py:402
  87.0 5.1 %collective-permute-start.1 = (f32[8,128]{1,0:T(8,128)S(1)}, f32[8,128]{1,0:T(8,128)S(1)}, u32[]{:S(2)}, u32[]{:S(2)}) collective-permute-start(f32[8,128]{1,0:T(8,128)S(1)} %norm_kernel.1.own_ref), channel_id=1, source_target_pairs={{0,2},{1,3},{2,0},{3,1},{4,6},{5,7},{6,4},{7,5},{8,10},{9,11},{10,... | collective-permute-start | bytes 12296 | tf_op jit(solution)/shard_map/ppermute | solution.py:402
  87.7 4.8 %collective-permute-start = (f32[8,128]{1,0:T(8,128)S(1)}, f32[8,128]{1,0:T(8,128)S(1)}, u32[]{:S(2)}, u32[]{:S(2)}) collective-permute-start(f32[8,128]{1,0:T(8,128)S(1)} %norm_kernel.1.own_ref), channel_id=1, source_target_pairs={{0,1},{1,2},{2,3},{3,0},{4,5},{5,6},{6,7},{7,4},{8,9},{9,10},{10,1... | collective-permute-start | bytes 12296 | tf_op jit(solution)/shard_map/ppermute | solution.py:402

commit v2 on v1

--- a/solution.py
+++ b/solution.py
@@ -17,7 +17,8 @@
 ORDER = DEGREE + 1
 CHUNK = 8
 MSG_ROWS = 6
-AHEAD = 5
+AHEAD = 12
+GROUP = 2
 
 f32 = jnp.float32
 bf16 = jnp.bfloat16
@@ -95,18 +96,30 @@
     lax.fori_loop(first, SWEEPS, sweep, 0)
 
 
-def write_message(gain_ref, msg_ref, extras):
+def quarters(ref, start):
+    for quarter in range(4):
+        tile = ref[start : start + DIRS, 128 * (quarter // 2) : 128 * (quarter // 2) + 128]
+        yield quarter, (tile, pltpu.roll(tile, 64, 1))
+
+
+def write_first(gain_ref, msg_ref, extras):
     low = iota((DIRS, 128), 1) < 64
     for f in range(LOCAL):
         for part in range(2):
-            start = part * PAIRS + f * DIRS
-            for quarter in range(4):
-                tile = gain_ref[start : start + DIRS, 128 * (quarter // 2) : 128 * (quarter // 2) + 128]
-                if quarter % 2:
-                    tile = pltpu.roll(tile, 64, 1)
-                if extras is not None:
-                    tile = jnp.where(low, tile, extras[f])
-                msg_ref[pl.ds(quarter * 32 + 2 * part + f, DIRS, stride=4), :] = tile
+            for quarter, tiles in quarters(gain_ref, part * PAIRS + f * DIRS):
+                msg_ref[pl.ds(quarter * 32 + 2 * part + f, DIRS, stride=4), :] = jnp.where(
+                    low, tiles[quarter % 2], extras[f]
+                )
+
+
+def write_packed(gain_ref, msg_ref):
+    low = iota((DIRS, 128), 1) < 64
+    for part in range(2):
+        starts = (part * PAIRS, part * PAIRS + DIRS)
+        for (quarter, one), (_, two) in zip(*(quarters(gain_ref, start) for start in starts)):
+            msg_ref[pl.ds(quarter * 16 + part, DIRS, stride=2), :] = jnp.where(
+                low, one[quarter % 2], two[1 - quarter % 2]
+            )
 
 
 def first_kernel(
@@ -138,11 +151,13 @@
         mask_ref[f] = jnp.where(apart, wide, 0.0)
     col_ref[...] = jnp.zeros(col_ref.shape, f32)
     for j in range(PAIRS):
-        for copy in copies(j):
-            copy.wait()
-        if j + AHEAD < PAIRS:
-            for copy in copies(j + AHEAD):
-                copy.start()
+        if j % GROUP == 0:
+            for i in range(j, j + GROUP):
+                for copy in copies(i):
+                    copy.wait()
+            for i in range(j + AHEAD, min(j + AHEAD + GROUP, PAIRS)):
+                for copy in copies(i):
+                    copy.start()
         for start in range(0, STATIONS, 16):
             rows = slice(start, start + 16)
             mask = mask_ref[j // DIRS, rows, :]
@@ -170,30 +185,32 @@
     extras = [
         jnp.where(lane < 96, weights[f], dest_ref[f].astype(f32)) for f in range(LOCAL)
     ]
-    write_message(gain_ref, msg_ref, extras)
+    write_first(gain_ref, msg_ref, extras)
 
 
 def second_kernel(
     re_ref, im_ref, sq_ref, start_ref, pen_ref, back_ref, msg_ref, gain_ref, target_ref, col_ref
 ):
     low = iota((DIRS, 128), 1) < 64
-    for f in range(LOCAL):
-        for part in range(2):
-            start = part * PAIRS + f * DIRS
-            for half in range(2):
-                first, second = (
-                    back_ref[pl.ds(quarter * 32 + 2 * part + f, DIRS, stride=4), :]
-                    for quarter in (2 * half, 2 * half + 1)
-                )
-                target_ref[start : start + DIRS, 128 * half : 128 * half + 128] = jnp.where(
-                    low, first, pltpu.roll(second, 64, 1)
-                )
+    for part in range(2):
+        for half in range(2):
+            first, second = (
+                back_ref[pl.ds(quarter * 16 + part, DIRS, stride=2), :]
+                for quarter in (2 * half, 2 * half + 1)
+            )
+            tiles = (
+                jnp.where(low, first, pltpu.roll(second, 64, 1)),
+                jnp.where(low, pltpu.roll(first, 64, 1), second),
+            )
+            for f in range(LOCAL):
+                start = part * PAIRS + f * DIRS
+                target_ref[start : start + DIRS, 128 * half : 128 * half + 128] = tiles[f]
     col_ref[...] = jnp.zeros(col_ref.shape, f32)
     pen = pen_ref[...]
     target_re, target_im = target_ref[:PAIRS], target_ref[PAIRS:]
     gain_ref[...] = start_ref[...]
     sweeps(0, (re_ref, im_ref, sq_ref), gain_ref, col_ref, target_re, target_im, pen)
-    write_message(gain_ref, msg_ref, None)
+    write_packed(gain_ref, msg_ref)
 
 
 def chebyshev(abscissa):
@@ -219,7 +236,9 @@
     return out
 
 
-def solve_kernel(x_ref, msg_ref, fresh_ref, coef_ref, inverse_ref, norm_ref):
+def solve_kernel(
+    x_ref, msg_ref, target_ref, fresh_ref, coef_ref, solver_ref, norm_ref
+):
     bands = x_ref.shape[0]
     low = iota((bands, 128), 1) < 64
     gains = jnp.where(low, x_ref[...], 0.0)
@@ -228,20 +247,41 @@
     coef = dot(rows, weight * gains)
     gram = dot(rows, weight * columns)
     row = iota((16, 128), 0)
-    inverse = (row == iota((16, 128), 1)).astype(f32)
-    for i in range(ORDER):
-        scale = 1.0 / gram[i : i + 1, i : i + 1]
-        factor = jnp.where(row == i, 0.0, gram[:, i : i + 1])
-        pivots = [m[i : i + 1, :] * scale for m in (coef, gram, inverse)]
-        coef, gram, inverse = (
-            jnp.where(row == i, pivot, m - factor * pivot)
-            for m, pivot in zip((coef, gram, inverse), pivots)
-        )
+    solved = (coef, gram, rows)
+    for i in range(0, ORDER, 2):
+        size = min(2, ORDER - i)
+        picked = [
+            jnp.broadcast_to(solved[1][:, i + n : i + n + 1], row.shape) for n in range(size)
+        ]
+        block = [[col[i + m : i + m + 1] for col in picked] for m in range(size)]
+        if size == 1:
+            inverse = [[1.0 / block[0][0]]]
+        else:
+            (p, q), (r, s) = block
+            scale = 1.0 / (p * s - q * r)
+            inverse = [[s * scale, -q * scale], [-r * scale, p * scale]]
+        inside = (row >= i) & (row < i + size)
+        factors = [jnp.where(inside, 0.0, col) for col in picked]
+        after = []
+        for m in solved:
+            pivots = [sum(inverse[a][n] * m[i + n : i + n + 1] for n in range(size)) for a in range(size)]
+            left = m - sum(factor * pivot for factor, pivot in zip(factors, pivots))
+            for n, pivot in enumerate(pivots):
+                left = jnp.where(row == i + n, pivot, left)
+            after.append(left)
+        solved = tuple(after)
+    coef, _, solver = solved
     fresh = dot(columns[:, :16], coef)
-    msg_ref[...] = 2.0 * fresh - gains
+    target_ref[...] = 2.0 * fresh - gains
+    owners = bands // LOCAL
+    msg_ref[...] = jnp.where(
+        iota((owners, 128), 1) < 64,
+        target_ref[pl.ds(0, owners, stride=2), :],
+        pltpu.roll(target_ref[pl.ds(1, owners, stride=2), :], 64, 1),
+    )
     fresh_ref[...] = fresh
     coef_ref[...] = coef
-    inverse_ref[...] = inverse
+    solver_ref[...] = solver
     start = jnp.where(lax.axis_index("band_2") == 0, 1.0, 0.0)
     primal = total(weight * (gains - fresh) ** 2)
     dual = total(jnp.where(low, weight * (fresh - start) ** 2, 0.0))
@@ -252,16 +292,18 @@
 
 
 def finish_kernel(
-    x_ref, target_ref, gain_ref, fresh_ref, coef_ref, inverse_ref, norm_ref, msg_ref,
-    coef_buf, rows_buf,
+    x_ref, target_ref, gain_ref, fresh_ref, coef_ref, solver_ref, norm_ref, msg_ref,
+    coef_buf, rows_buf, gain_buf,
 ):
     bands = x_ref.shape[0]
     owners = bands // 2
     low = iota((bands, 128), 1) < 64
     weight = x_ref[:, 64:65]
-    gains = jnp.where(low, gain_ref[...], 0.0)
-    columns, rows = basis_columns(bands), basis_rows(bands)
-    change = dot(inverse_ref[:, :16], dot(rows, weight * (gains - target_ref[...])))
+    gain_buf[pl.ds(0, owners, stride=2), :] = gain_ref[...]
+    gain_buf[pl.ds(1, owners, stride=2), :] = pltpu.roll(gain_ref[...], 64, 1)
+    gains = jnp.where(low, gain_buf[...], 0.0)
+    columns = basis_columns(bands)
+    change = dot(solver_ref[...], weight * (gains - target_ref[...]))
     step = dot(columns[:, :16], change)
     fresh = fresh_ref[...] + step
     primal = total(weight * (gains - fresh) ** 2)
@@ -379,23 +421,27 @@
         limit=20 << 20,
     )
     held = exchange(message)
-    target, fresh, coef, inverse, norms = call(
+    owners = bands // LOCAL
+    message, *kept = call(
         solve_kernel,
-        [shape(bands, 128), shape(bands, 128), shape(16, 128), shape(16, 128), shape(8, 128)],
+        [
+            shape(owners, 128), shape(bands, 128), shape(bands, 128), shape(16, 128),
+            shape(16, 128), shape(8, 128),
+        ],
         held,
     )
-    back = exchange(target)
     rows = pltpu.VMEM((2 * PAIRS, STATIONS), f32)
     message = call(
-        second_kernel, shape(bands, 128), *state, back,
+        second_kernel, shape(owners, 128), *state, exchange(message),
         scratch=[rows, rows, columns],
     )
+    target, *kept = kept
+    spread = pltpu.VMEM((bands, 128), f32)
     message = call(
-        finish_kernel, shape(MSG_ROWS * bands // LOCAL, 128),
-        held, target, exchange(message), fresh, coef, inverse, norms,
-        scratch=[pltpu.VMEM((16, 128), f32), pltpu.VMEM((bands, 128), f32)],
-    )
-    everything = exchange(message.reshape(bands // LOCAL, 1, MSG_ROWS * 128)).reshape(-1, 128)
+        finish_kernel, shape(MSG_ROWS * owners, 128), held, target, exchange(message), *kept,
+        scratch=[pltpu.VMEM((16, 128), f32), spread, spread],
+    )
+    everything = exchange(message.reshape(owners, 1, MSG_ROWS * 128)).reshape(-1, 128)
     norms = call(norm_kernel, shape(8, 128), everything)
     count = lax.axis_size("dir")
     others = [

time: 93.4 us -> 91.8 us (0.983)
  Pallas kernels: 21.7 us -> 20.7 us
where the time goes in v2:
time: 91.8 us; the launch traced here: 91.5 us
  blocking collectives  62.4 us (68%)
  Pallas kernels  20.7 us (23%)
  starting transfers between devices  4.63 us (5%)
  waiting for transfers between devices  3.07 us (3%)
    all_to_all x4, blocking collectives, exchange(): lax.all_to_all(message, BAND, split_axis=0, concat_axis=0, tiled=True)  62.4 us
    pallas_call x7, Pallas kernels, call(): pl.pallas_call(kernel, out_shape=outs, in_specs=in_specs, scratch_shapes=...  20.7 us
    ppermute x3, starting transfers between devices, per_device(): lax.ppermute(norms, 'dir', [(i, (i + step) % count) for i in range(count)])  4.63 us
    ppermute x3, waiting for transfers between devices, per_device(): lax.ppermute(norms, 'dir', [(i, (i + step) % count) for i in range(count)])  3.07 us
  transfers between devices with their start and end apart: 3, of which 2 were waited for; matrix products, arithmetic and copies ran while one was open for 0% of the time, Pallas kernels for 1%

profile of v2, /device:TPU:6, one launch (start us, length us, event | category | flops | bytes accessed | tf_op | source)
XLA Modules:
  0.0 91.5 jit_solution(18313844762816464391)
XLA Ops:
  0.6 10.0 %first_kernel.1 = (f32[16,256,256]{2,1,0:T(8,128)S(1)}, f32[16,256,256]{2,1,0:T(8,128)S(1)}, f32[16,256,256]{2,1,0:T(8,128)S(1)}, f32[32,256]{1,0:T(8,128)S(1)},...) custom-call(s32[2,8,8]{2,1,0:T(8,128)} %flags_in.1, s32[2]{0:T(128)} %dest_in.1, bf16[2,8,2,256,256]{4,3,2,1,0:T(8,128)(2,1)} %vis_ref.1, ...), custom_call_target="tpu_custom_call" | custom-call | tf_op jit(solution)/shard_map/first_kernel/pallas_call | solution.py:385
  10.7 19.7 %all_to_all.38 = f32[64,2,128]{2,1,0:T(2,128)S(1)} all-to-all(f32[64,2,128]{2,1,0:T(2,128)S(1)} %bitcast.20), channel_id=1, replica_groups=mesh['band_0'=4,'band_1'=8,'band_2'=2,'dir'=4] {'band_0','band_1','band_2'}, dimensions={0} | all-to-all | bytes 131072 | tf_op jit(solution)/shard_map/all_to_all | solution.py:400
  30.4 1.2 %solve_kernel.1 = (f32[64,128]{1,0:T(8,128)S(1)}, f32[128,128]{1,0:T(8,128)S(1)}, f32[128,128]{1,0:T(8,128)S(1)}, f32[16,128]{1,0:T(8,128)S(1)}, f32[16,128]{1,0:T(8,128)S(1)}, /*index=5*/f32[8,128]{1,0:T(8,128)S(1)}) custom-call(f32[128,128]{1,0:T(8,128)S(1)} %bitcast.15), custom_call_target="tpu_custom_call" | custom-call | tf_op jit(solution)/shard_map/solve_kernel/pallas_call | solution.py:385
  31.6 13.5 %all_to_all.39 = f32[64,1,128]{2,1,0:T(1,128)S(1)} all-to-all(f32[64,1,128]{2,1,0:T(1,128)S(1)} %bitcast.21), channel_id=1, replica_groups=mesh['band_0'=4,'band_1'=8,'band_2'=2,'dir'=4] {'band_0','band_1','band_2'}, dimensions={0} | all-to-all | bytes 65536 | tf_op jit(solution)/shard_map/all_to_all | solution.py:400
  45.1 7.3 %second_kernel.1 = f32[64,128]{1,0:T(8,128)S(1)} custom-call(f32[16,256,256]{2,1,0:T(8,128)S(1)} %get-tuple-element.19.re_ref, f32[16,256,256]{2,1,0:T(8,128)S(1)} %get-tuple-element.20.im_ref, f32[16,256,256]{2,1,0:T(8,128)S(1)} %get-tuple-element.21.sq_ref, f32[32,256]{1,0:T(8,128)S(1)} %get-tuple-element.22.start_ref, ...), custom_call_target="tpu_custom_call" | custom-call | tf_op jit(solution)/shard_map/second_kernel/pallas_call | solution.py:385
  52.3 13.3 %all_to_all.40 = f32[64,1,128]{2,1,0:T(1,128)S(1)} all-to-all(f32[64,1,128]{2,1,0:T(1,128)S(1)} %bitcast.18), channel_id=1, replica_groups=mesh['band_0'=4,'band_1'=8,'band_2'=2,'dir'=4] {'band_0','band_1','band_2'}, dimensions={0} | all-to-all | bytes 65536 | tf_op jit(solution)/shard_map/all_to_all | solution.py:400
  65.7 0.8 finish_kernel.1
  66.4 15.9 %all_to_all.41 = f32[64,1,768]{2,1,0:T(1,128)S(1)} all-to-all(f32[64,1,768]{2,1,0:T(1,128)S(1)} %bitcast.14), channel_id=1, replica_groups=mesh['band_0'=4,'band_1'=8,'band_2'=2,'dir'=4] {'band_0','band_1','band_2'}, dimensions={0} | all-to-all | bytes 393216 | tf_op jit(solution)/shard_map/all_to_all | solution.py:400
  82.4 0.1 norm_kernel.1.own_ref
  82.5 3.0 %collective-permute-start.2 = (f32[8,128]{1,0:T(8,128)S(1)}, f32[8,128]{1,0:T(8,128)S(1)}, u32[]{:S(2)}, u32[]{:S(2)}) collective-permute-start(f32[8,128]{1,0:T(8,128)S(1)} %norm_kernel.1.own_ref), channel_id=1, source_target_pairs={{0,3},{1,0},{2,1},{3,2},{4,7},{5,4},{6,5},{7,6},{8,11},{9,8},{10,9... | collective-permute-start | bytes 12296 | tf_op jit(solution)/shard_map/ppermute | solution.py:448
  85.5 0.6 collective-permute-start.1
  86.1 1.0 %collective-permute-start = (f32[8,128]{1,0:T(8,128)S(1)}, f32[8,128]{1,0:T(8,128)S(1)}, u32[]{:S(2)}, u32[]{:S(2)}) collective-permute-start(f32[8,128]{1,0:T(8,128)S(1)} %norm_kernel.1.own_ref), channel_id=1, source_target_pairs={{0,1},{1,2},{2,3},{3,0},{4,5},{5,6},{6,7},{7,4},{8,9},{9,10},{10,1... | collective-permute-start | bytes 12296 | tf_op jit(solution)/shard_map/ppermute | solution.py:448
  87.1 0.8 assemble_kernel.1
  87.9 0.0 collective-permute-done.2.third_ref
  87.9 2.7 %collective-permute-done.1.second_ref = f32[8,128]{1,0:T(8,128)S(1)} collective-permute-done((f32[8,128]{1,0:T(8,128)S(1)}, f32[8,128]{1,0:T(8,128)S(1)}, u32[]{:S(2)}, u32[]{:S(2)}) %collective-permute-start.1) | collective-permute-done | bytes 4128 | tf_op jit(solution)/shard_map/ppermute | solution.py:448
  90.6 0.3 collective-permute-done.first_ref
  90.9 0.6 total_kernel.1
Async XLA Ops:
  82.5 5.4 %collective-permute-start.2 = (f32[8,128]{1,0:T(8,128)S(1)}, f32[8,128]{1,0:T(8,128)S(1)}, u32[]{:S(2)}, u32[]{:S(2)}) collective-permute-start(f32[8,128]{1,0:T(8,128)S(1)} %norm_kernel.1.own_ref), channel_id=1, source_target_pairs={{0,3},{1,0},{2,1},{3,2},{4,7},{5,4},{6,5},{7,6},{8,11},{9,8},{10,9... | collective-permute-start | bytes 12296 | tf_op jit(solution)/shard_map/ppermute | solution.py:448
  85.5 5.1 %collective-permute-start.1 = (f32[8,128]{1,0:T(8,128)S(1)}, f32[8,128]{1,0:T(8,128)S(1)}, u32[]{:S(2)}, u32[]{:S(2)}) collective-permute-start(f32[8,128]{1,0:T(8,128)S(1)} %norm_kernel.1.own_ref), channel_id=1, source_target_pairs={{0,2},{1,3},{2,0},{3,1},{4,6},{5,7},{6,4},{7,5},{8,10},{9,11},{10,... | collective-permute-start | bytes 12296 | tf_op jit(solution)/shard_map/ppermute | solution.py:448
  86.1 4.8 %collective-permute-start = (f32[8,128]{1,0:T(8,128)S(1)}, f32[8,128]{1,0:T(8,128)S(1)}, u32[]{:S(2)}, u32[]{:S(2)}) collective-permute-start(f32[8,128]{1,0:T(8,128)S(1)} %norm_kernel.1.own_ref), channel_id=1, source_target_pairs={{0,1},{1,2},{2,3},{3,0},{4,5},{5,6},{6,7},{7,4},{8,9},{9,10},{10,1... | collective-permute-start | bytes 12296 | tf_op jit(solution)/shard_map/ppermute | solution.py:448

commit v3 on v2

--- a/solution.py
+++ b/solution.py
@@ -17,7 +17,6 @@
 ORDER = DEGREE + 1
 CHUNK = 8
 MSG_ROWS = 6
-AHEAD = 12
 GROUP = 2
 
 f32 = jnp.float32
@@ -137,7 +136,7 @@
     dest_copy = pltpu.make_async_copy(dest_in, dest_ref, sems.at[1, PAIRS])
     flags_copy.start()
     dest_copy.start()
-    for j in range(AHEAD):
+    for j in range(PAIRS):
         for copy in copies(j):
             copy.start()
     flags_copy.wait()
@@ -148,23 +147,20 @@
     apart = iota((STATIONS, STATIONS), 0) != iota((STATIONS, STATIONS), 1)
     for f in range(LOCAL):
         wide = matrix_dot(matrix_dot(spread, keep[f].astype(bf16)).astype(bf16), across)
-        mask_ref[f] = jnp.where(apart, wide, 0.0)
+        mask_ref[f] = jnp.where(apart, wide, 0.0).astype(bf16)
     col_ref[...] = jnp.zeros(col_ref.shape, f32)
     for j in range(PAIRS):
-        if j % GROUP == 0:
-            for i in range(j, j + GROUP):
+        if j < GROUP or j % GROUP == 0:
+            for i in range(j, j + (1 if j < GROUP else GROUP)):
                 for copy in copies(i):
                     copy.wait()
-            for i in range(j + AHEAD, min(j + AHEAD + GROUP, PAIRS)):
-                for copy in copies(i):
-                    copy.start()
         for start in range(0, STATIONS, 16):
             rows = slice(start, start + 16)
             mask = mask_ref[j // DIRS, rows, :]
             data_re = vis_buf[j, 0, rows, :].astype(f32)
             data_im = vis_buf[j, 1, rows, :].astype(f32)
-            model_re = mask * sky_buf[j, 0, rows, :].astype(f32)
-            model_im = mask * sky_buf[j, 1, rows, :].astype(f32)
+            model_re = (mask * sky_buf[j, 0, rows, :]).astype(f32)
+            model_im = (mask * sky_buf[j, 1, rows, :]).astype(f32)
             a_re = model_re * data_re + model_im * data_im
             a_im = model_re * data_im - model_im * data_re
             sq = model_re * model_re + model_im * model_im
@@ -244,8 +240,8 @@
     gains = jnp.where(low, x_ref[...], 0.0)
     weight = x_ref[:, 64:65]
     columns, rows = basis_columns(bands), basis_rows(bands)
-    coef = dot(rows, weight * gains)
-    gram = dot(rows, weight * columns)
+    both = dot(rows, weight * jnp.concatenate([gains, columns], axis=1))
+    coef, gram = both[:, :128], both[:, 128:]
     row = iota((16, 128), 0)
     solved = (coef, gram, rows)
     for i in range(0, ORDER, 2):
@@ -415,7 +411,7 @@
         in_specs=[HBM] * 4,
         scratch=[
             pltpu.VMEM(rfi_flags.shape, jnp.int32), pltpu.SMEM(destination.shape, jnp.int32),
-            halves, halves, pltpu.VMEM((LOCAL, STATIONS, STATIONS), f32), columns,
+            halves, halves, pltpu.VMEM((LOCAL, STATIONS, STATIONS), bf16), columns,
             pltpu.SemaphoreType.DMA((2, PAIRS + 1)),
         ],
         limit=20 << 20,

time: 91.8 us -> 91.6 us (level)
  no operation moved by 1% of the time
where the time goes in v3:
time: 91.6 us; the launch traced here: 91.3 us
  blocking collectives  62.4 us (68%)
  Pallas kernels  20.5 us (22%)
  starting transfers between devices  4.62 us (5%)
  waiting for transfers between devices  3.07 us (3%)
    all_to_all x4, blocking collectives, exchange(): lax.all_to_all(message, BAND, split_axis=0, concat_axis=0, tiled=True)  62.4 us
    pallas_call x7, Pallas kernels, call(): pl.pallas_call(kernel, out_shape=outs, in_specs=in_specs, scratch_shapes=...  20.5 us
    ppermute x3, starting transfers between devices, per_device(): lax.ppermute(norms, 'dir', [(i, (i + step) % count) for i in range(count)])  4.62 us
    ppermute x3, waiting for transfers between devices, per_device(): lax.ppermute(norms, 'dir', [(i, (i + step) % count) for i in range(count)])  3.07 us
  transfers between devices with their start and end apart: 3, of which 2 were waited for; matrix products, arithmetic and copies ran while one was open for 0% of the time, Pallas kernels for 1%

profile of v3, /device:TPU:6, one launch (start us, length us, event | category | flops | bytes accessed | tf_op | source)
XLA Modules:
  0.0 91.3 jit_solution(8801708178252142908)
XLA Ops:
  0.6 9.8 %first_kernel.1 = (f32[16,256,256]{2,1,0:T(8,128)S(1)}, f32[16,256,256]{2,1,0:T(8,128)S(1)}, f32[16,256,256]{2,1,0:T(8,128)S(1)}, f32[32,256]{1,0:T(8,128)S(1)},...) custom-call(s32[2,8,8]{2,1,0:T(8,128)} %flags_in.1, s32[2]{0:T(128)} %dest_in.1, bf16[2,8,2,256,256]{4,3,2,1,0:T(8,128)(2,1)} %vis_ref.1, ...), custom_call_target="tpu_custom_call" | custom-call | tf_op jit(solution)/shard_map/first_kernel/pallas_call | solution.py:381
  10.5 19.7 %all_to_all.38 = f32[64,2,128]{2,1,0:T(2,128)S(1)} all-to-all(f32[64,2,128]{2,1,0:T(2,128)S(1)} %bitcast.20), channel_id=1, replica_groups=mesh['band_0'=4,'band_1'=8,'band_2'=2,'dir'=4] {'band_0','band_1','band_2'}, dimensions={0} | all-to-all | bytes 131072 | tf_op jit(solution)/shard_map/all_to_all | solution.py:396
  30.2 1.2 %solve_kernel.1 = (f32[64,128]{1,0:T(8,128)S(1)}, f32[128,128]{1,0:T(8,128)S(1)}, f32[128,128]{1,0:T(8,128)S(1)}, f32[16,128]{1,0:T(8,128)S(1)}, f32[16,128]{1,0:T(8,128)S(1)}, /*index=5*/f32[8,128]{1,0:T(8,128)S(1)}) custom-call(f32[128,128]{1,0:T(8,128)S(1)} %bitcast.15), custom_call_target="tpu_custom_call" | custom-call | tf_op jit(solution)/shard_map/solve_kernel/pallas_call | solution.py:381
  31.4 13.5 %all_to_all.39 = f32[64,1,128]{2,1,0:T(1,128)S(1)} all-to-all(f32[64,1,128]{2,1,0:T(1,128)S(1)} %bitcast.21), channel_id=1, replica_groups=mesh['band_0'=4,'band_1'=8,'band_2'=2,'dir'=4] {'band_0','band_1','band_2'}, dimensions={0} | all-to-all | bytes 65536 | tf_op jit(solution)/shard_map/all_to_all | solution.py:396
  44.9 7.3 %second_kernel.1 = f32[64,128]{1,0:T(8,128)S(1)} custom-call(f32[16,256,256]{2,1,0:T(8,128)S(1)} %get-tuple-element.19.re_ref, f32[16,256,256]{2,1,0:T(8,128)S(1)} %get-tuple-element.20.im_ref, f32[16,256,256]{2,1,0:T(8,128)S(1)} %get-tuple-element.21.sq_ref, f32[32,256]{1,0:T(8,128)S(1)} %get-tuple-element.22.start_ref, ...), custom_call_target="tpu_custom_call" | custom-call | tf_op jit(solution)/shard_map/second_kernel/pallas_call | solution.py:381
  52.1 13.3 %all_to_all.40 = f32[64,1,128]{2,1,0:T(1,128)S(1)} all-to-all(f32[64,1,128]{2,1,0:T(1,128)S(1)} %bitcast.18), channel_id=1, replica_groups=mesh['band_0'=4,'band_1'=8,'band_2'=2,'dir'=4] {'band_0','band_1','band_2'}, dimensions={0} | all-to-all | bytes 65536 | tf_op jit(solution)/shard_map/all_to_all | solution.py:396
  65.4 0.8 finish_kernel.1
  66.2 15.9 %all_to_all.41 = f32[64,1,768]{2,1,0:T(1,128)S(1)} all-to-all(f32[64,1,768]{2,1,0:T(1,128)S(1)} %bitcast.14), channel_id=1, replica_groups=mesh['band_0'=4,'band_1'=8,'band_2'=2,'dir'=4] {'band_0','band_1','band_2'}, dimensions={0} | all-to-all | bytes 393216 | tf_op jit(solution)/shard_map/all_to_all | solution.py:396
  82.2 0.1 norm_kernel.1.own_ref
  82.2 3.0 %collective-permute-start.2 = (f32[8,128]{1,0:T(8,128)S(1)}, f32[8,128]{1,0:T(8,128)S(1)}, u32[]{:S(2)}, u32[]{:S(2)}) collective-permute-start(f32[8,128]{1,0:T(8,128)S(1)} %norm_kernel.1.own_ref), channel_id=1, source_target_pairs={{0,3},{1,0},{2,1},{3,2},{4,7},{5,4},{6,5},{7,6},{8,11},{9,8},{10,9... | collective-permute-start | bytes 12296 | tf_op jit(solution)/shard_map/ppermute | solution.py:444
  85.3 0.6 collective-permute-start.1
  85.9 1.0 %collective-permute-start = (f32[8,128]{1,0:T(8,128)S(1)}, f32[8,128]{1,0:T(8,128)S(1)}, u32[]{:S(2)}, u32[]{:S(2)}) collective-permute-start(f32[8,128]{1,0:T(8,128)S(1)} %norm_kernel.1.own_ref), channel_id=1, source_target_pairs={{0,1},{1,2},{2,3},{3,0},{4,5},{5,6},{6,7},{7,4},{8,9},{9,10},{10,1... | collective-permute-start | bytes 12296 | tf_op jit(solution)/shard_map/ppermute | solution.py:444
  86.9 0.8 assemble_kernel.1
  87.6 0.0 collective-permute-done.2.third_ref
  87.6 2.7 %collective-permute-done.1.second_ref = f32[8,128]{1,0:T(8,128)S(1)} collective-permute-done((f32[8,128]{1,0:T(8,128)S(1)}, f32[8,128]{1,0:T(8,128)S(1)}, u32[]{:S(2)}, u32[]{:S(2)}) %collective-permute-start.1) | collective-permute-done | bytes 4128 | tf_op jit(solution)/shard_map/ppermute | solution.py:444
  90.4 0.3 collective-permute-done.first_ref
  90.7 0.6 total_kernel.1
Async XLA Ops:
  82.2 5.4 %collective-permute-start.2 = (f32[8,128]{1,0:T(8,128)S(1)}, f32[8,128]{1,0:T(8,128)S(1)}, u32[]{:S(2)}, u32[]{:S(2)}) collective-permute-start(f32[8,128]{1,0:T(8,128)S(1)} %norm_kernel.1.own_ref), channel_id=1, source_target_pairs={{0,3},{1,0},{2,1},{3,2},{4,7},{5,4},{6,5},{7,6},{8,11},{9,8},{10,9... | collective-permute-start | bytes 12296 | tf_op jit(solution)/shard_map/ppermute | solution.py:444
  85.3 5.1 %collective-permute-start.1 = (f32[8,128]{1,0:T(8,128)S(1)}, f32[8,128]{1,0:T(8,128)S(1)}, u32[]{:S(2)}, u32[]{:S(2)}) collective-permute-start(f32[8,128]{1,0:T(8,128)S(1)} %norm_kernel.1.own_ref), channel_id=1, source_target_pairs={{0,2},{1,3},{2,0},{3,1},{4,6},{5,7},{6,4},{7,5},{8,10},{9,11},{10,... | collective-permute-start | bytes 12296 | tf_op jit(solution)/shard_map/ppermute | solution.py:444
  85.9 4.8 %collective-permute-start = (f32[8,128]{1,0:T(8,128)S(1)}, f32[8,128]{1,0:T(8,128)S(1)}, u32[]{:S(2)}, u32[]{:S(2)}) collective-permute-start(f32[8,128]{1,0:T(8,128)S(1)} %norm_kernel.1.own_ref), channel_id=1, source_target_pairs={{0,1},{1,2},{2,3},{3,0},{4,5},{5,6},{6,7},{7,4},{8,9},{9,10},{10,1... | collective-permute-start | bytes 12296 | tf_op jit(solution)/shard_map/ppermute | solution.py:444
